TPU v7x, 32 devices: a whole 2x2x4 slice. The times are simulated.
32 devices in a mesh: row: 8 (over z, x), col: 4 (over y, core).
Axes of the slice: x: 2, y: 2, z: 4, core: 2. Of those that a mesh axis runs over, the one named last changes fastest.
Arguments:
- grad: bfloat16 [16384, 1024], P(('row', 'col')), may hold values from -2500 to 2500
- left_root: bfloat16 [16384, 1024], P(('row', 'col')), may hold values from -0.051 to 3, as said below
- right_root: bfloat16 [16384, 1024], P(('row', 'col')), may hold values from -0.051 to 3, as said below
Outputs:
- update: bfloat16 [16384, 1024], P(('row', 'col'))
Inputs may be any that keep to these rules, and one draw needn't show every extreme that they name: `left_root`: each block L_b is symmetric and positive definite. `right_root`: each block R_b is symmetric and positive definite.
All inputs are finite; a program needn't handle non-finite values.
Results may differ from a plain program's by a relative error of at most 0.0049.
Values may be sent and summed in bfloat16 or wider, within the bound.
A program may use at most 64 MiB of HBM per device.

v0:
```python
import jax
import jax.numpy as jnp
from jax import lax
from jax.sharding import PartitionSpec as P

BLK = 1024
epsilon = 1e-06
clip_rms = 1.0


def partner(shard, axis, distance):
    return lax.ppermute(shard, axis, [(i, i ^ 1 << distance) for i in range(lax.axis_size(axis))])


def apply_right(gradient_rows, own_start, other_start, rows_here, right_root, partner_right):
    own_cols = lax.dynamic_slice_in_dim(gradient_rows, own_start, rows_here, 1)
    other_cols = lax.dynamic_slice_in_dim(gradient_rows, other_start, rows_here, 1)
    applied = jnp.dot(own_cols, right_root, preferred_element_type=jnp.float32)
    applied = applied + jnp.dot(other_cols, partner_right, preferred_element_type=jnp.float32)
    return applied.astype(jnp.bfloat16)


def shards(grad, left_root, right_root):
    rows_here = grad.shape[0]
    parity = lax.axis_index("col") % 2
    own_start = parity * rows_here
    other_start = (1 - parity) * rows_here
    partner_right = partner(right_root, "col", 0)
    right_applied = apply_right(grad, own_start, other_start, rows_here, right_root, partner_right)
    partner_rows = partner(right_applied, "col", 0)
    own_left = lax.dynamic_slice_in_dim(left_root, own_start, rows_here, 1)
    other_left = lax.dynamic_slice_in_dim(left_root, other_start, rows_here, 1)
    preconditioned = jnp.dot(own_left, right_applied, preferred_element_type=jnp.float32)
    preconditioned = preconditioned + jnp.dot(
        other_left, partner_rows, preferred_element_type=jnp.float32
    )
    grad_sq = jnp.sum(jnp.square(grad.astype(jnp.float32)))
    cond_sq = jnp.sum(preconditioned * preconditioned)
    global_sq = lax.psum(grad_sq, ("row", "col"))
    partner_sums = partner(jnp.stack([grad_sq, cond_sq]), "col", 0)
    block_grad = grad_sq + partner_sums[0]
    block_cond = cond_sq + partner_sums[1]
    block_count = BLK * BLK
    total_count = lax.axis_size("row") * lax.axis_size("col") // 2 * block_count
    clip_factor = clip_rms / jnp.sqrt(global_sq / total_count + epsilon)
    graft_ratio = jnp.sqrt(
        (block_grad / block_count + epsilon) / (block_cond / block_count + epsilon)
    )
    return (clip_factor * graft_ratio * preconditioned).astype(jnp.bfloat16)


def solution(mesh):
    placed = (P(("row", "col"), None), P(("row", "col"), None), P(("row", "col"), None))
    return jax.shard_map(
        shards, mesh=mesh, in_specs=placed, out_specs=P(("row", "col"), None), check_vma=False
    )
```

profile of v0, /device:TPU:0, one launch (start us, length us, event | category | flops | bytes accessed | tf_op | source)
XLA Modules:
  0.0 59.8 jit_solution(16291145906748680650)
XLA Ops:
  0.0 0.0 copy-start
  0.0 0.0 copy-start.1
  0.0 0.5 collective-permute-start
  0.5 2.1 %fusion.2 = f32[512,1024]{1,0:T(8,128)S(1)} fusion(bf16[512,1024]{1,0:T(8,128)(2,1)} %param.5, bf16[512,1024]{1,0:T(8,128)(2,1)} %param.3, s32[]{:T(128)S(6)} %select_n.16), kind=kOutput, calls=%fused_computation.7 | convolution fusion | flops 536870912 | bytes 3670020 | tf_op jit(solution)/shard_map/dot_general | solution.py:18
  2.6 0.5 collective-permute-done
  3.1 0.0 copy-done.1
  3.1 2.0 %add_convert_fusion = bf16[512,1024]{1,0:T(8,128)(2,1)S(1)} fusion(f32[512,1024]{1,0:T(8,128)S(1)} %fusion.2, bf16[512,1024]{1,0:T(8,128)(2,1)} %collective-permute-done, bf16[512,1024]{1,0:T(8,128)(2,1)S(1)} %copy-done.1, s32[]{:T(128)S(6)} %select_n.17), kind=kOutput, calls=%fused_computation.2 | convolution fusion | flops 537919488 | bytes 4718596 | tf_op jit(solution)/shard_map/dot_general | solution.py:19
  5.1 0.4 collective-permute-start.1
  5.5 1.2 %multiply_reduce_fusion.1 = f32[]{:T(128)} fusion(bf16[512,1024]{1,0:T(8,128)(2,1)S(1)} %copy-done.1), kind=kLoop, calls=%fused_computation.3 | loop fusion | flops 1572863 | bytes 1048580 | tf_op jit(solution)/shard_map/reduce_sum | solution.py:37
  6.7 41.8 %psum.7 = f32[]{:T(128)} all-reduce(f32[]{:T(128)} %multiply_reduce_fusion.1), channel_id=1, replica_groups=mesh['row'=8,'col'=4] {'row','col'}, use_global_device_ids=true, to_apply=%region_1.2 | all-reduce | flops 1 | bytes 8 | tf_op jit(solution)/shard_map/psum | solution.py:39
  49.3 0.0 copy-done
  49.3 0.7 %fusion.4 = f32[512,1024]{1,0:T(8,128)S(1)} fusion(bf16[512,1024]{1,0:T(8,128)(2,1)S(1)} %add_convert_fusion, bf16[512,1024]{1,0:T(8,128)(2,1)S(1)} %copy-done, s32[]{:T(128)S(6)} %select_n.16), kind=kOutput, calls=%fused_computation.9 | convolution fusion | flops 536870912 | bytes 3670020 | tf_op jit(solution)/shard_map/dot_general | solution.py:33
  50.0 0.0 collective-permute-done.1
  50.0 2.7 %multiply_reduce_fusion = (f32[]{:T(128)}, f32[512,1024]{1,0:T(8,128)S(1)}) fusion(f32[512,1024]{1,0:T(8,128)S(1)} %fusion.4, bf16[512,1024]{1,0:T(8,128)(2,1)} %collective-permute-done.1, bf16[512,1024]{1,0:T(8,128)(2,1)S(1)} %copy-done, s32[]{:T(128)S(6)} %select_n.17), kind=kOutput, calls=%fused_computation.1 | convolution fusion | flops 538443776 | bytes 5767176 | tf_op jit(solution)/shard_map/dot_general | solution.py:34
  52.7 1.4 %pad_maximum_fusion = f32[2]{0:T(128)S(1)} fusion(f32[1]{0:T(128)} %bitcast.1, f32[1]{0:T(128)} %bitcast), kind=kLoop, calls=%fused_computation.15 | loop fusion | flops 2 | bytes 16 | tf_op jit(solution)/shard_map/stack | solution.py:40
  54.1 0.0 collective-permute-start.2
  54.1 1.1 %collective-permute-done.2 = f32[2]{0:T(128)S(1)} collective-permute-done((f32[2]{0:T(128)S(1)}, f32[2]{0:T(128)S(1)}, u32[]{:S(2)}, u32[]{:S(2)}) %collective-permute-start.2) | collective-permute-done | bytes 40 | tf_op jit(solution)/shard_map/ppermute | solution.py:12
  55.3 0.7 %fusion.10 = (f32[1]{0:T(128)}, f32[1]{0:T(128)}) fusion(f32[2]{0:T(128)S(1)} %collective-permute-done.2), kind=kLoop, calls=%fused_computation.16 | loop fusion | bytes 16 | tf_op jit(solution)/shard_map/slice | solution.py:42
  58.6 1.2 %multiply_convert_fusion = bf16[512,1024]{1,0:T(8,128)(2,1)} fusion(f32[512,1024]{1,0:T(8,128)S(1)} %get-tuple-element.8, f32[]{:T(128)S(6)} %mul.21), kind=kLoop, calls=%fused_computation | loop fusion | flops 1048576 | bytes 3145732 | tf_op jit(solution)/shard_map/convert_element_type | solution.py:49
Async XLA Ops:
  0.0 49.3 %copy-start = (bf16[512,1024]{1,0:T(8,128)(2,1)S(1)}, bf16[512,1024]{1,0:T(8,128)(2,1)}, u32[]{:S(2)}) copy-start(bf16[512,1024]{1,0:T(8,128)(2,1)} %param.4) | copy-start | bytes 3145732
  0.0 3.1 %copy-start.1 = (bf16[512,1024]{1,0:T(8,128)(2,1)S(1)}, bf16[512,1024]{1,0:T(8,128)(2,1)}, u32[]{:S(2)}) copy-start(bf16[512,1024]{1,0:T(8,128)(2,1)} %param.3) | copy-start | bytes 3145732
  0.0 3.1 %collective-permute-start = (bf16[512,1024]{1,0:T(8,128)(2,1)}, bf16[512,1024]{1,0:T(8,128)(2,1)}, u32[]{:S(2)}, u32[]{:S(2)}) collective-permute-start(bf16[512,1024]{1,0:T(8,128)(2,1)} %param.5), channel_id=1, source_target_pairs={{0,1},{1,0},{2,3},{3,2},{4,5},{5,4},{6,7},{7,6},{8,9},{9,8},{10,11... | collective-permute-start | bytes 3145736 | tf_op jit(solution)/shard_map/ppermute | solution.py:12
  5.1 44.9 %collective-permute-start.1 = (bf16[512,1024]{1,0:T(8,128)(2,1)S(1)}, bf16[512,1024]{1,0:T(8,128)(2,1)}, u32[]{:S(2)}, u32[]{:S(2)}) collective-permute-start(bf16[512,1024]{1,0:T(8,128)(2,1)S(1)} %add_convert_fusion), channel_id=1, source_target_pairs={{0,1},{1,0},{2,3},{3,2},{4,5},{5,4},{6,7},{7,6},{8,9},{9,8},{10,11... | collective-permute-start | bytes 3145736 | tf_op jit(solution)/shard_map/ppermute | solution.py:12
  54.1 1.2 %collective-permute-start.2 = (f32[2]{0:T(128)S(1)}, f32[2]{0:T(128)S(1)}, u32[]{:S(2)}, u32[]{:S(2)}) collective-permute-start(f32[2]{0:T(128)S(1)} %pad_maximum_fusion), channel_id=1, source_target_pairs={{0,1},{1,0},{2,3},{3,2},{4,5},{5,4},{6,7},{7,6},{8,9},{9,8},{10,11... | collective-permute-start | bytes 32 | tf_op jit(solution)/shard_map/ppermute | solution.py:12
where the time goes:
time: 60.2 us; the launch traced here: 59.8 us
  blocking collectives  41.8 us (69%)
  matrix products  7.48 us (12%)
  other arithmetic  3.84 us (6%)
  between operations  3.42 us (6%)
  waiting for transfers between devices  1.68 us (3%)
  starting transfers between devices  0.94 us (2%)
  local copies, waits for them, and re-layouts  0.67 us (1%)
    psum x1, blocking collectives, shards(): global_sq = lax.psum(grad_sq, ('row', 'col'))  41.8 us
    dot_general x1, matrix products, shards(): jnp.dot(other_left, partner_rows, preferred_element_type=jnp.float32)  2.71 us
    dot_general x1, matrix products, apply_right(): applied = jnp.dot(own_cols, right_root, preferred_element_type=jnp.float32)  2.1 us
    dot_general x1, matrix products, apply_right(): jnp.dot(other_cols, partner_right, preferred_element_type=jnp.float32)  1.96 us
    ppermute x3, waiting for transfers between devices, partner(): lax.ppermute(shard, axis, [(i, i ^ 1 << distance) for i in range(lax.axis...  1.68 us
    another operation x1, other arithmetic, shards(): partner_sums = partner(jnp.stack([grad_sq, cond_sq]), 'col', 0)  1.41 us
    convert_element_type x1, other arithmetic, shards(): return (clip_factor * graft_ratio * preconditioned).astype(jnp.bfloat16)  1.22 us
    reduce_sum x1, other arithmetic, shards(): grad_sq = jnp.sum(jnp.square(grad.astype(jnp.float32)))  1.21 us
  transfers between devices with their start and end apart: 3, of which 2 were waited for; matrix products, arithmetic and copies ran while one was open for 7% of the time, Pallas kernels for 0%

commit v1 on v0

--- a/solution.py
+++ b/solution.py
@@ -36,7 +36,7 @@
     )
     grad_sq = jnp.sum(jnp.square(grad.astype(jnp.float32)))
     cond_sq = jnp.sum(preconditioned * preconditioned)
-    global_sq = lax.psum(grad_sq, ("row", "col"))
+    global_sq = jax.lax.psum(jax.lax.psum(grad_sq, "col"), "row")
     partner_sums = partner(jnp.stack([grad_sq, cond_sq]), "col", 0)
     block_grad = grad_sq + partner_sums[0]
     block_cond = cond_sq + partner_sums[1]

time: 60.2 us -> 49.5 us (0.82)
  blocking collectives: 41.8 us -> 31.1 us
    psum x1 -> x2, blocking collectives: 41.8 us -> 31.1 us  [shards(): global_sq = jax.lax.psum(jax.lax.psum(grad_sq, 'col'), 'row')]
  transfers between devices with their start and end apart: 3 -> 3, of which waited for: 2 -> 2; matrix products, arithmetic and copies ran while one was open for 7% -> 8% of each run, Pallas kernels for 0% -> 0%
where the time goes in v1:
time: 49.5 us; the launch traced here: 49.2 us
  blocking collectives  31.1 us (63%)
  matrix products  7.48 us (15%)
  other arithmetic  3.84 us (8%)
  between operations  3.42 us (7%)
  waiting for transfers between devices  1.68 us (3%)
  starting transfers between devices  0.94 us (2%)
  local copies, waits for them, and re-layouts  0.67 us (1%)
    psum x2, blocking collectives, shards(): global_sq = jax.lax.psum(jax.lax.psum(grad_sq, 'col'), 'row')  31.1 us
    dot_general x1, matrix products, shards(): jnp.dot(other_left, partner_rows, preferred_element_type=jnp.float32)  2.71 us
    dot_general x1, matrix products, apply_right(): applied = jnp.dot(own_cols, right_root, preferred_element_type=jnp.float32)  2.1 us
    dot_general x1, matrix products, apply_right(): jnp.dot(other_cols, partner_right, preferred_element_type=jnp.float32)  1.96 us
    ppermute x3, waiting for transfers between devices, partner(): lax.ppermute(shard, axis, [(i, i ^ 1 << distance) for i in range(lax.axis...  1.68 us
    another operation x1, other arithmetic, shards(): partner_sums = partner(jnp.stack([grad_sq, cond_sq]), 'col', 0)  1.41 us
    convert_element_type x1, other arithmetic, shards(): return (clip_factor * graft_ratio * preconditioned).astype(jnp.bfloat16)  1.22 us
    reduce_sum x1, other arithmetic, shards(): grad_sq = jnp.sum(jnp.square(grad.astype(jnp.float32)))  1.21 us
  transfers between devices with their start and end apart: 3, of which 2 were waited for; matrix products, arithmetic and copies ran while one was open for 8% of the time, Pallas kernels for 0%

profile of v1, /device:TPU:0, one launch (start us, length us, event | category | flops | bytes accessed | tf_op | source)
XLA Modules:
  0.0 49.2 jit_solution(11049162301493636608)
XLA Ops:
  0.0 0.0 copy-start
  0.0 0.0 copy-start.1
  0.0 0.5 %collective-permute-start = (bf16[512,1024]{1,0:T(8,128)(2,1)}, bf16[512,1024]{1,0:T(8,128)(2,1)}, u32[]{:S(2)}, u32[]{:S(2)}) collective-permute-start(bf16[512,1024]{1,0:T(8,128)(2,1)} %param.5), channel_id=1, source_target_pairs={{0,1},{1,0},{2,3},{3,2},{4,5},{5,4},{6,7},{7,6},{8,9},{9,8},{10,11... | collective-permute-start | bytes 3145736 | tf_op jit(solution)/shard_map/ppermute | solution.py:12
  0.5 2.1 %fusion.2 = f32[512,1024]{1,0:T(8,128)S(1)} fusion(bf16[512,1024]{1,0:T(8,128)(2,1)} %param.5, bf16[512,1024]{1,0:T(8,128)(2,1)} %param.3, s32[]{:T(128)S(6)} %select_n.16), kind=kOutput, calls=%fused_computation.7 | convolution fusion | flops 536870912 | bytes 3670020 | tf_op jit(solution)/shard_map/dot_general | solution.py:18
  2.6 0.5 %collective-permute-done = bf16[512,1024]{1,0:T(8,128)(2,1)} collective-permute-done((bf16[512,1024]{1,0:T(8,128)(2,1)}, bf16[512,1024]{1,0:T(8,128)(2,1)}, u32[]{:S(2)}, u32[]{:S(2)}) %collective-permute-start) | collective-permute-done | bytes 1048608 | tf_op jit(solution)/shard_map/ppermute | solution.py:12
  3.1 0.0 copy-done.1
  3.1 2.0 %add_convert_fusion = bf16[512,1024]{1,0:T(8,128)(2,1)S(1)} fusion(f32[512,1024]{1,0:T(8,128)S(1)} %fusion.2, bf16[512,1024]{1,0:T(8,128)(2,1)} %collective-permute-done, bf16[512,1024]{1,0:T(8,128)(2,1)S(1)} %copy-done.1, s32[]{:T(128)S(6)} %select_n.17), kind=kOutput, calls=%fused_computation.2 | convolution fusion | flops 537919488 | bytes 4718596 | tf_op jit(solution)/shard_map/dot_general | solution.py:19
  5.1 0.4 collective-permute-start.1
  5.5 1.2 %multiply_reduce_fusion.1 = f32[]{:T(128)} fusion(bf16[512,1024]{1,0:T(8,128)(2,1)S(1)} %copy-done.1), kind=kLoop, calls=%fused_computation.3 | loop fusion | flops 1572863 | bytes 1048580 | tf_op jit(solution)/shard_map/reduce_sum | solution.py:37
  6.7 8.9 %psum.14 = f32[]{:T(128)} all-reduce(f32[]{:T(128)} %multiply_reduce_fusion.1), channel_id=1, replica_groups=mesh['row'=8,'col'=4] {'col'}, use_global_device_ids=true, to_apply=%region_1.2 | all-reduce | flops 1 | bytes 8 | tf_op jit(solution)/shard_map/psum | solution.py:39
  15.6 22.3 %psum.15 = f32[]{:T(128)} all-reduce(f32[]{:T(128)} %psum.14), channel_id=1, replica_groups=mesh['row'=8,'col'=4] {'row'}, use_global_device_ids=true, to_apply=%region_2.3 | all-reduce | flops 1 | bytes 8 | tf_op jit(solution)/shard_map/psum | solution.py:39
  38.6 0.0 copy-done
  38.6 0.7 %fusion.4 = f32[512,1024]{1,0:T(8,128)S(1)} fusion(bf16[512,1024]{1,0:T(8,128)(2,1)S(1)} %add_convert_fusion, bf16[512,1024]{1,0:T(8,128)(2,1)S(1)} %copy-done, s32[]{:T(128)S(6)} %select_n.16), kind=kOutput, calls=%fused_computation.9 | convolution fusion | flops 536870912 | bytes 3670020 | tf_op jit(solution)/shard_map/dot_general | solution.py:33
  39.3 0.0 collective-permute-done.1
  39.3 2.7 %multiply_reduce_fusion = (f32[]{:T(128)}, f32[512,1024]{1,0:T(8,128)S(1)}) fusion(f32[512,1024]{1,0:T(8,128)S(1)} %fusion.4, bf16[512,1024]{1,0:T(8,128)(2,1)} %collective-permute-done.1, bf16[512,1024]{1,0:T(8,128)(2,1)S(1)} %copy-done, s32[]{:T(128)S(6)} %select_n.17), kind=kOutput, calls=%fused_computation.1 | convolution fusion | flops 538443776 | bytes 5767176 | tf_op jit(solution)/shard_map/dot_general | solution.py:34
  42.0 1.4 %pad_maximum_fusion = f32[2]{0:T(128)S(1)} fusion(f32[1]{0:T(128)} %bitcast.1, f32[1]{0:T(128)} %bitcast), kind=kLoop, calls=%fused_computation.15 | loop fusion | flops 2 | bytes 16 | tf_op jit(solution)/shard_map/stack | solution.py:40
  43.4 0.0 collective-permute-start.2
  43.5 1.1 %collective-permute-done.2 = f32[2]{0:T(128)S(1)} collective-permute-done((f32[2]{0:T(128)S(1)}, f32[2]{0:T(128)S(1)}, u32[]{:S(2)}, u32[]{:S(2)}) %collective-permute-start.2) | collective-permute-done | bytes 40 | tf_op jit(solution)/shard_map/ppermute | solution.py:12
  44.6 0.7 %fusion.10 = (f32[1]{0:T(128)}, f32[1]{0:T(128)}) fusion(f32[2]{0:T(128)S(1)} %collective-permute-done.2), kind=kLoop, calls=%fused_computation.16 | loop fusion | bytes 16 | tf_op jit(solution)/shard_map/slice | solution.py:42
  47.9 1.2 %multiply_convert_fusion = bf16[512,1024]{1,0:T(8,128)(2,1)} fusion(f32[512,1024]{1,0:T(8,128)S(1)} %get-tuple-element.8, f32[]{:T(128)S(6)} %mul.21), kind=kLoop, calls=%fused_computation | loop fusion | flops 1048576 | bytes 3145732 | tf_op jit(solution)/shard_map/convert_element_type | solution.py:49
Async XLA Ops:
  0.0 38.6 %copy-start = (bf16[512,1024]{1,0:T(8,128)(2,1)S(1)}, bf16[512,1024]{1,0:T(8,128)(2,1)}, u32[]{:S(2)}) copy-start(bf16[512,1024]{1,0:T(8,128)(2,1)} %param.4) | copy-start | bytes 3145732
  0.0 3.1 %copy-start.1 = (bf16[512,1024]{1,0:T(8,128)(2,1)S(1)}, bf16[512,1024]{1,0:T(8,128)(2,1)}, u32[]{:S(2)}) copy-start(bf16[512,1024]{1,0:T(8,128)(2,1)} %param.3) | copy-start | bytes 3145732
  0.0 3.1 %collective-permute-start = (bf16[512,1024]{1,0:T(8,128)(2,1)}, bf16[512,1024]{1,0:T(8,128)(2,1)}, u32[]{:S(2)}, u32[]{:S(2)}) collective-permute-start(bf16[512,1024]{1,0:T(8,128)(2,1)} %param.5), channel_id=1, source_target_pairs={{0,1},{1,0},{2,3},{3,2},{4,5},{5,4},{6,7},{7,6},{8,9},{9,8},{10,11... | collective-permute-start | bytes 3145736 | tf_op jit(solution)/shard_map/ppermute | solution.py:12
  5.1 34.2 %collective-permute-start.1 = (bf16[512,1024]{1,0:T(8,128)(2,1)S(1)}, bf16[512,1024]{1,0:T(8,128)(2,1)}, u32[]{:S(2)}, u32[]{:S(2)}) collective-permute-start(bf16[512,1024]{1,0:T(8,128)(2,1)S(1)} %add_convert_fusion), channel_id=1, source_target_pairs={{0,1},{1,0},{2,3},{3,2},{4,5},{5,4},{6,7},{7,6},{8,9},{9,8},{10,11... | collective-permute-start | bytes 3145736 | tf_op jit(solution)/shard_map/ppermute | solution.py:12
  43.4 1.2 %collective-permute-start.2 = (f32[2]{0:T(128)S(1)}, f32[2]{0:T(128)S(1)}, u32[]{:S(2)}, u32[]{:S(2)}) collective-permute-start(f32[2]{0:T(128)S(1)} %pad_maximum_fusion), channel_id=1, source_target_pairs={{0,1},{1,0},{2,3},{3,2},{4,5},{5,4},{6,7},{7,6},{8,9},{9,8},{10,11... | collective-permute-start | bytes 32 | tf_op jit(solution)/shard_map/ppermute | solution.py:12
